TPU v7x, 32 devices: a whole 2x2x4 slice. The times are simulated.
32 devices in a mesh: term: 8 (over z, core), sector: 4 (over y, x).
Axes of the slice: x: 2, y: 2, z: 4, core: 2. Of those that a mesh axis runs over, the one named last changes fastest.
Arguments:
- wavefunction: bfloat16 [24, 256, 256], P('sector'), may hold values from -6 to 6
- left_env: bfloat16 [24, 24, 256, 256], P('term', 'sector')
- right_env: bfloat16 [24, 24, 256, 256], P('term', 'sector')
- source: int32 [24, 24], P('term'), may hold values from 0 to 23, as said below
- block_size: int32 [24, 2], P('sector'), may hold values from 32 to 256
Outputs:
- first_product: float32 [24, 256, 256], P('sector', 'term')
- second_product: float32 [24, 256, 256], P('sector', 'term')
Inputs may be any that keep to these rules, and one draw needn't show every extreme that they name: Owner of sector s is s // 6. Among the 3 x 6 entries of source in one device's rows (one index of term) and columns (one index of sector), at most 5 name sectors of any one owner, and some owner is named exactly 5 times.
All inputs are finite; a program needn't handle non-finite values.
Results may differ from a plain program's by a relative error of at most 0.0037.
Values may be sent and summed in bfloat16 or wider, within the bound.
A program may use at most 64 MiB of HBM per device.

v0:
```python
import jax
import jax.numpy as jnp
from jax import lax
from jax.sharding import PartitionSpec as P

epsilon = 1e-06


def block_mask(block_size, width):
    positions = jnp.arange(width, dtype=jnp.int32)
    row_keep = positions[None, :] < block_size[:, 0:1]
    column_keep = positions[None, :] < block_size[:, 1:2]
    return row_keep[:, :, None] & column_keep[:, None, :]


def fetch_blocks(masked, source):
    local_count = masked.shape[0]
    width = masked.shape[1]
    bond_count = source.shape[0]
    my_index = lax.axis_index("sector")
    item_count = bond_count * local_count
    wanted = lax.dynamic_slice_in_dim(source, my_index * local_count, local_count, 1).reshape(
        item_count
    )
    pieces = lax.all_gather(masked, "sector", axis=0, tiled=True)
    piece_count = pieces.shape[0]
    numbers = jnp.arange(piece_count, dtype=jnp.int32)
    onehot = (wanted[:, None] == numbers[None, :]).astype(jnp.bfloat16)
    picked = jnp.dot(
        onehot, pieces.reshape(piece_count, width * width), preferred_element_type=jnp.float32
    )
    return picked.astype(jnp.bfloat16).reshape(bond_count, local_count, width, width)


def apply_operator(vector, left_env, right_env, source, keep):
    masked = jnp.where(keep, vector, jnp.zeros_like(vector))
    picked = fetch_blocks(masked, source)
    half_product = jnp.einsum(
        "bkij,bkjl->bkil", left_env, picked, preferred_element_type=jnp.float32
    ).astype(jnp.bfloat16)
    bond_terms = jnp.einsum(
        "bkil,bkml->bkim", half_product, right_env, preferred_element_type=jnp.float32
    )
    summed = jnp.sum(bond_terms, axis=0)
    return (jnp.where(keep, summed, jnp.zeros_like(summed)), masked)


def body(wavefunction, left_env, right_env, source, block_size):
    width = wavefunction.shape[1]
    keep = block_mask(block_size, width)
    term_count = lax.axis_size("term")
    term_index = lax.axis_index("term")
    row_count = width // term_count
    total_count = lax.axis_size("sector") * wavefunction.shape[0] * width * width
    partial_value, masked = apply_operator(wavefunction, left_env, right_env, source, keep)
    masked_float = masked.astype(jnp.float32)
    whole_sum = lax.psum(partial_value, "term")
    first_product = lax.dynamic_slice_in_dim(whole_sum, term_index * row_count, row_count, 1)
    margin, self_norm = lax.psum(
        (jnp.sum(masked_float * whole_sum), jnp.sum(masked_float * masked_float)), "sector"
    )
    residual = whole_sum - margin / self_norm * masked_float
    spread = lax.psum(jnp.sum(residual * residual), "sector")
    next_vector = (residual * lax.rsqrt(spread / total_count + epsilon)).astype(jnp.bfloat16)
    second_partial, _ = apply_operator(next_vector, left_env, right_env, source, keep)
    second_product = lax.psum_scatter(second_partial, "term", scatter_dimension=1, tiled=True)
    return (first_product, second_product)


def solution(mesh):
    placed = (
        P("sector", None, None),
        P("term", "sector", None, None),
        P("term", "sector", None, None),
        P("term", None),
        P("sector", None),
    )
    return jax.shard_map(
        body,
        mesh=mesh,
        in_specs=placed,
        out_specs=(P("sector", "term", None), P("sector", "term", None)),
        check_vma=False,
    )
```

profile of v0, /device:TPU:0, one launch (start us, length us, event | category | flops | bytes accessed | tf_op | source)
XLA Modules:
  0.0 256.0 jit_solution(13237176541998194756)
XLA Ops:
  7.2 0.9 slice_bitcast_fusion.1
  8.2 2.3 and_select_fusion.3
  10.7 0.1 eq.8
  10.8 46.5 %all-gather.3.cloned.1.call-done = bf16[24,256,256]{2,1,0:T(8,128)(2,1)} async-done(((bf16[6,256,256]{2,1,0:T(8,128)(2,1)}), bf16[24,256,256]{2,1,0:T(8,128)(2,1)}) %all-gather.3.cloned.1.call-update) | async-done | bytes 3145744 | tf_op jit(solution)/shard_map/all_gather | solution.py:25
  57.3 3.7 %copy.16 = bf16[3,8,256,256]{3,1,2,0:T(8,128)(2,1)S(1)} copy(bf16[3,8,256,256]{3,2,1,0:T(8,128)(2,1)} %bitcast.40) | data formatting | bytes 6291456
  60.9 1.0 convolution_convert_fusion.1
  62.0 0.7 copy.17
  62.7 1.7 slice.11
  64.4 5.0 %and_select_fusion.2 = f32[6,256,256]{2,1,0:T(8,128)} fusion(bf16[3,6,256,256]{3,2,1,0:T(8,128)(2,1)S(1)} %copy-done, bf16[3,6,256,256]{3,2,1,0:T(8,128)(2,1)} %bitcast.43, bf16[3,6,256,256]{3,2,1,0:T(8,128)(2,1)} %param.6, pred[6,256]{1,0:T(8,128)(4,1)S(1)} %get-tuple-element.8, pred[6,256]{1,0:T(8,128)(4,1)S(1)} %get-tuple-element.9), kind=kOutput, calls=%fused_computation.4 | convolution fusion | flops 1209925632 | bytes 8653824 | tf_op jit(solution)/shard_map/bkil,bkml->bkim/dot_general | solution.py:41
  69.5 62.0 %all-reduce.3.cloned.1.call-done = f32[6,256,256]{2,1,0:T(8,128)} async-done(((f32[6,256,256]{2,1,0:T(8,128)}), f32[6,256,256]{2,1,0:T(8,128)}) %all-reduce.3.cloned.1.call-update) | async-done | bytes 1572880 | tf_op jit(solution)/shard_map/psum | solution.py:57
  131.5 2.6 %fusion.25 = (f32[]{:T(128)}, f32[]{:T(128)}) fusion(f32[6,256,256]{2,1,0:T(8,128)} %all-reduce.3.cloned.1.call-done, bf16[6,256,256]{2,1,0:T(8,128)(2,1)S(1)} %copy-done.1, pred[6,256]{1,0:T(8,128)(4,1)S(1)} %get-tuple-element.8, pred[6,256]{1,0:T(8,128)(4,1)S(1)} %get-tuple-element.9), kind=kLoop, calls=%fused_computation.24 | loop fusion | flops 2752510 | bytes 2362376 | tf_op jit(solution)/shard_map/reduce_sum | solution.py:60
  134.1 10.4 %all-reduce = (f32[]{:T(128)}, f32[]{:T(128)}) all-reduce(f32[]{:T(128)} %get-tuple-element.3, f32[]{:T(128)} %get-tuple-element.2), channel_id=1, replica_groups=mesh['term'=8,'sector'=4] {'sector'}, use_global_device_ids=true, to_apply=%region_2.3 | all-reduce | flops 2 | bytes 16 | tf_op jit(solution)/shard_map/psum | solution.py:59
  145.9 2.6 %multiply_reduce_fusion = f32[]{:T(128)} fusion(f32[6,256,256]{2,1,0:T(8,128)} %all-reduce.3.cloned.1.call-done, f32[]{:T(128)S(6)} %div.6, bf16[6,256,256]{2,1,0:T(8,128)(2,1)S(1)} %copy-done.1, pred[6,256]{1,0:T(8,128)(4,1)S(1)} %get-tuple-element.8, pred[6,256]{1,0:T(8,128)(4,1)S(1)} %get-tuple-element.9), kind=kLoop, calls=%fused_computation.27 | loop fusion | flops 2752511 | bytes 2362376 | tf_op jit(solution)/shard_map/reduce_sum | solution.py:63
  148.5 8.6 %psum.31 = f32[]{:T(128)} all-reduce(f32[]{:T(128)} %multiply_reduce_fusion), channel_id=1, replica_groups=mesh['term'=8,'sector'=4] {'sector'}, use_global_device_ids=true, to_apply=%region_6.7 | all-reduce | flops 1 | bytes 8 | tf_op jit(solution)/shard_map/psum | solution.py:63
  157.8 2.8 %and_select_fusion.1 = bf16[6,256,256]{2,1,0:T(8,128)(2,1)} fusion(f32[6,256,256]{2,1,0:T(8,128)} %all-reduce.3.cloned.1.call-done, f32[]{:T(128)S(6)} %rsqrt.3, f32[]{:T(128)S(6)} %div.6, pred[6,256]{1,0:T(8,128)(4,1)S(1)} %get-tuple-element.8, pred[6,256]{1,0:T(8,128)(4,1)S(1)} %get-tuple-element.9, bf16[6,256,256]{2,1,0:T(8,128)(2,1)S(1)} %copy-done.1), kind=kLoop, calls=%fused_computation.3 | loop fusion | flops 3145728 | bytes 3148808 | tf_op jit(solution)/shard_map/jit(_where)/select_n | solution.py:36
  160.6 0.2 reduce-scatter.2.cloned.1.call-start
  160.8 42.1 %all-gather.5.cloned.1.call-done = bf16[24,256,256]{2,1,0:T(8,128)(2,1)} async-done(((bf16[6,256,256]{2,1,0:T(8,128)(2,1)}), bf16[24,256,256]{2,1,0:T(8,128)(2,1)}) %all-gather.5.cloned.1.call-update) | async-done | bytes 3145744 | tf_op jit(solution)/shard_map/all_gather | solution.py:25
  203.0 3.7 %copy.18 = bf16[3,8,256,256]{3,1,2,0:T(8,128)(2,1)S(1)} copy(bf16[3,8,256,256]{3,2,1,0:T(8,128)(2,1)} %bitcast.41) | data formatting | bytes 6291456
  206.6 1.0 convolution_convert_fusion
  207.7 0.7 copy.19
  208.4 1.7 slice.12
  210.1 4.9 %and_select_fusion = f32[6,256,256]{2,1,0:T(8,128)} fusion(bf16[3,6,256,256]{3,2,1,0:T(8,128)(2,1)S(1)} %copy-done, bf16[3,6,256,256]{3,2,1,0:T(8,128)(2,1)} %bitcast.42, bf16[3,6,256,256]{3,2,1,0:T(8,128)(2,1)} %param.6, pred[6,256]{1,0:T(8,128)(4,1)S(1)} %get-tuple-element.8, pred[6,256]{1,0:T(8,128)(4,1)S(1)} %get-tuple-element.9), kind=kOutput, calls=%fused_computation.2 | convolution fusion | flops 1209925632 | bytes 8653824 | tf_op jit(solution)/shard_map/bkil,bkml->bkim/dot_general | solution.py:41
  215.0 1.6 constant_dynamic-slice_fusion
  216.7 32.8 %reduce-scatter.2.cloned.1.call-done = f32[6,32,256]{2,1,0:T(8,128)} async-done(((f32[6,256,256]{2,1,0:T(8,128)}), f32[6,32,256]{2,1,0:T(8,128)}) %reduce-scatter.2.cloned.1.call-update) | async-done | bytes 196624 | tf_op jit(solution)/shard_map/reduce_scatter | solution.py:66
  (15 shorter events, 0.4 us)
Async XLA Ops:
  7.2 57.2 %copy-start = (bf16[3,6,256,256]{3,2,1,0:T(8,128)(2,1)S(1)}, bf16[3,6,256,256]{3,2,1,0:T(8,128)(2,1)}, u32[]{:S(2)}) copy-start(bf16[3,6,256,256]{3,2,1,0:T(8,128)(2,1)} %param.7) | copy-start | bytes 7077892
  7.2 3.4 %copy-start.2 = (s32[3,24]{1,0:T(4,128)S(1)}, s32[3,24]{1,0:T(4,128)}, u32[]{:S(2)}) copy-start(s32[3,24]{1,0:T(4,128)} %param.8) | copy-start | bytes 868
  7.2 50.1 %all-gather.3.cloned.1.call-start = ((), (), s32[]{:S(2)}) async-start(), calls=%async_computation.1 | async-start | bytes 3932160 | tf_op jit(solution)/shard_map/all_gather | solution.py:25
  10.5 120.9 %all-reduce.3.cloned.1.call-start = ((), (), s32[]{:S(2)}) async-start(), calls=%async_computation.2 | async-start | bytes 3145728 | tf_op jit(solution)/shard_map/psum | solution.py:57
  64.4 67.1 %copy-start.1 = (bf16[6,256,256]{2,1,0:T(8,128)(2,1)S(1)}, bf16[6,256,256]{2,1,0:T(8,128)(2,1)}, u32[]{:S(2)}) copy-start(bf16[6,256,256]{2,1,0:T(8,128)(2,1)} %param.5) | copy-start | bytes 2359300
  69.4 133.6 %all-gather.5.cloned.1.call-start = ((), (), s32[]{:S(2)}) async-start(), calls=%async_computation.3 | async-start | bytes 3932160 | tf_op jit(solution)/shard_map/all_gather | solution.py:25
  160.6 88.8 %reduce-scatter.2.cloned.1.call-start = ((), (), s32[]{:S(2)}) async-start(), calls=%async_computation.4 | async-start | bytes 1769472 | tf_op jit(solution)/shard_map/reduce_scatter | solution.py:66
Sparse Core Ops, SparseCore 0:
  10.7 46.5 all-gather.2
  69.5 61.8 all-reduce.2
  160.7 42.1 all-gather.4
  215.1 34.2 reduce-scatter.1
where the time goes:
time: 256 us
  waiting for transfers between devices  183 us (71%)
  blocking collectives  19 us (7%)
  between operations  15.9 us (6%)
  local copies, waits for them, and re-layouts  14.8 us (6%)
  matrix products  12 us (5%)
  other arithmetic  10.5 us (4%)
    all_gather x2, waiting for transfers between devices, fetch_blocks(): pieces = lax.all_gather(masked, 'sector', axis=0, tiled=True)  88.6 us
    psum x1, waiting for transfers between devices, body(): whole_sum = lax.psum(partial_value, 'term')  62 us
    reduce_scatter x1, waiting for transfers between devices, body(): lax.psum_scatter(second_partial, 'term', scatter_dimension=1, tiled=True)  32.8 us
    unnamed x12, local copies, waits for them, and re-layouts  12.1 us
    psum x1, blocking collectives, body(): lax.psum((jnp.sum(masked_float * whole_sum), jnp.sum(masked_float * maske...  10.4 us
    dot_general x2, matrix products, apply_operator(): jnp.einsum('bkil,bkml->bkim', half_product, right_env, preferred_element_...  9.96 us
    psum x1, blocking collectives, body(): spread = lax.psum(jnp.sum(residual * residual), 'sector')  8.58 us
    select_n x2, other arithmetic, apply_operator(): masked = jnp.where(keep, vector, jnp.zeros_like(vector))  5.17 us
  transfers between devices with their start and end apart: 4, of which 4 were waited for; matrix products, arithmetic and copies ran while one was open for 1% of the time, Pallas kernels for 0%

commit v1 on v0

v1 whole, which is shorter than its diff:
```python
import functools

import jax
import jax.numpy as jnp
from jax import lax
from jax.experimental import pallas as pl
from jax.experimental.pallas import tpu as pltpu
from jax.sharding import PartitionSpec as P

epsilon = 1e-06
MESH = pl.DeviceIdType.MESH
LANES = 128


def grid_of(sector_count):
    across = 1
    while across * across * 2 <= sector_count:
        across *= 2
    while sector_count % across:
        across -= 1
    return across, sector_count // across


def fold(values):
    rows = values.reshape(-1, 8, values.shape[-1])
    total = jnp.sum(rows, axis=0)
    parts = [total[:, i : i + LANES] for i in range(0, total.shape[1], LANES)]
    return functools.reduce(lambda a, b: a + b, parts)


def kernel(
    dims,
    source_ref,
    size_ref,
    wave_hbm,
    left_hbm,
    right_hbm,
    first_ref,
    second_ref,
    wave,
    left,
    right,
    pool,
    partial,
    from_core,
    chip_sum,
    from_line,
    term_out,
    term_in,
    sector_out,
    sector_in,
    load_sem,
    send_sem,
    net_sem,
    core_sem,
    pair_send,
    pair_recv,
    line_send,
    line_recv,
    term_send,
    term_recv,
    sector_send,
    sector_recv,
):
    terms, sectors, blocks, bonds, width = dims
    line = terms // 2
    rows = width // terms
    group = 2 if blocks % 2 == 0 else 1
    groups = blocks // group
    nx, ny = grid_of(sectors)
    t = lax.axis_index("term")
    s = lax.axis_index("sector")
    c = lax.rem(t, 2)
    z = lax.div(t, 2)
    x = lax.rem(s, nx)
    y = lax.div(s, nx)
    other = t + 1 - 2 * c

    def sector_at(a, b):
        if nx == ny:
            dx = a * (1 - c) + b * c
            dy = b * (1 - c) + a * c
        else:
            dx, dy = a, b
        return lax.rem(y + dy, ny) * nx + lax.rem(x + dx, nx)

    def z_at(j):
        return lax.rem(z + j, line)

    loads = [
        pltpu.make_async_copy(wave_hbm, wave, load_sem.at[0]),
        pltpu.make_async_copy(left_hbm, left, load_sem.at[1]),
        pltpu.make_async_copy(right_hbm, right, load_sem.at[2]),
    ]
    for copy in loads:
        copy.start()

    barrier = pltpu.get_barrier_semaphore()
    for j in range(1, terms):
        pl.semaphore_signal(
            barrier, inc=1, device_id=(lax.rem(t + j, terms), s), device_id_type=MESH
        )
    for j in range(1, sectors):
        pl.semaphore_signal(
            barrier, inc=1, device_id=(t, lax.rem(s + j, sectors)), device_id_type=MESH
        )

    row_at = lax.broadcasted_iota(jnp.int32, (width, width), 0)
    column_at = lax.broadcasted_iota(jnp.int32, (width, width), 1)

    def keep_of(k):
        return (row_at < size_ref[k, 0]) & (column_at < size_ref[k, 1])

    loads[0].wait()
    for k in range(blocks):
        pool[0, s * blocks + k] = jnp.where(keep_of(k), wave[k], jnp.zeros_like(wave[k]))

    pl.semaphore_wait(barrier, terms + sectors - 2)

    sent = []

    def send(stage, region, slot, target, by_core):
        number = len(sent)
        copy = pltpu.make_async_remote_copy(
            src_ref=region,
            dst_ref=region,
            send_sem=send_sem.at[number],
            recv_sem=(core_sem if by_core else net_sem).at[stage, slot],
            device_id=target,
            device_id_type=MESH,
        )
        copy.start()
        sent.append(copy)

    def arrived(stage, region, slot, by_core):
        pltpu.make_async_remote_copy(
            src_ref=region,
            dst_ref=region,
            send_sem=send_sem.at[0],
            recv_sem=(core_sem if by_core else net_sem).at[stage, slot],
            device_id=(other, s),
            device_id_type=MESH,
        ).wait_recv()

    def gather(stage, region_of, z_order):
        def spread_out(piece, zz, to_first, to_second, to_core):
            region = region_of(piece, zz, c)
            slot = zz * sectors + piece
            if to_second:
                for b in range(1, ny):
                    send(stage, region, slot, (t, sector_at(0, b)), False)
            if to_first:
                for a in range(1, nx):
                    send(stage, region, slot, (t, sector_at(a, 0)), False)
            if to_core:
                send(stage, region, slot, (other, s), True)

        def land(piece, zz):
            arrived(stage, region_of(piece, zz, c), zz * sectors + piece, False)

        def firsts(j):
            for a in range(1, nx):
                piece = sector_at(a, 0)
                land(piece, z_at(j))
                spread_out(piece, z_at(j), False, True, True)

        def seconds(j):
            for a in range(nx):
                for b in range(1, ny):
                    piece = sector_at(a, b)
                    land(piece, z_at(j))
                    spread_out(piece, z_at(j), False, False, True)

        for i, j in enumerate(z_order):
            if i == 0:
                for jj in z_order[1:]:
                    region = region_of(s, z, c)
                    send(stage, region, z * sectors + s, (2 * z_at(jj) + c, s), False)
                spread_out(s, z, True, True, len(z_order) > 1)
            else:
                land(s, z_at(j))
                spread_out(s, z_at(j), True, True, True)
                firsts(z_order[i - 1])
        firsts(z_order[-1])
        for j in z_order:
            seconds(j)
        for j in z_order:
            for a in range(nx):
                for b in range(ny):
                    if a or b or len(z_order) > 1:
                        piece = sector_at(a, b)
                        arrived(
                            stage,
                            region_of(piece, z_at(j), 1 - c),
                            z_at(j) * sectors + piece,
                            True,
                        )
        for copy in sent:
            copy.wait_send()
        sent.clear()

    def wave_region(piece, zz, core):
        half = width // 2
        return pool.at[
            0, pl.ds(piece * blocks, blocks), pl.ds(pl.multiple_of(core * half, half), half), :
        ]

    def next_region(piece, zz, core):
        return pool.at[
            1,
            pl.ds(piece * blocks, blocks),
            pl.ds(pl.multiple_of((2 * zz + core) * rows, rows), rows),
            :,
        ]

    def pair_copy(stage, g):
        span = pl.ds(g * group, group)
        return pltpu.make_async_remote_copy(
            src_ref=partial.at[stage, span, :, 1 - c],
            dst_ref=from_core.at[stage, span],
            send_sem=pair_send.at[stage, g],
            recv_sem=pair_recv.at[stage, g],
            device_id=(other, s),
            device_id_type=MESH,
        )

    def line_copy(stage, g, j):
        span = pl.ds(g * group, group)
        return pltpu.make_async_remote_copy(
            src_ref=chip_sum.at[stage, z_at(j), span],
            dst_ref=from_line.at[stage, z, span],
            send_sem=line_send.at[stage, g, j],
            recv_sem=line_recv.at[stage, g, z],
            device_id=(2 * z_at(j) + c, s),
            device_id_type=MESH,
        )

    def line_landed(stage, g, j):
        span = pl.ds(g * group, group)
        pltpu.make_async_remote_copy(
            src_ref=chip_sum.at[stage, z, span],
            dst_ref=from_line.at[stage, z_at(j), span],
            send_sem=line_send.at[stage, g, j],
            recv_sem=line_recv.at[stage, g, z_at(j)],
            device_id=(2 * z_at(j) + c, s),
            device_id_type=MESH,
        ).wait_recv()

    def operate(stage, with_sums):
        def finish(g):
            pair_copy(stage, g).wait_recv()
            for i in range(group):
                k = g * group + i
                both = partial[stage, k, :, pl.ds(c, 1)].reshape(line, rows, width)
                both = both + from_core[stage, k]
                chip_sum[stage, :, k] = both.astype(jnp.bfloat16)
            for j in range(1, line):
                line_copy(stage, g, j).start()

        def step(g, sums):
            for i in range(group):
                k = g * group + i
                total = None
                for b in range(bonds):
                    picked = pool[stage, source_ref[b, s * blocks + k]]
                    half = jnp.dot(
                        left[b, k], picked, preferred_element_type=jnp.float32
                    ).astype(jnp.bfloat16)
                    term = lax.dot_general(
                        half,
                        right[b, k],
                        (((1,), (1,)), ((), ())),
                        preferred_element_type=jnp.float32,
                    )
                    total = term if total is None else total + term
                total = jnp.where(keep_of(k), total, jnp.zeros_like(total))
                if with_sums:
                    own = pool[0, s * blocks + k].astype(jnp.float32)
                    sums = (sums[0] + fold(total * own), sums[1] + fold(total * total))
                partial[stage, k] = total.reshape(line, 2, rows, width)
            pair_copy(stage, g).start()

            @pl.when(g > 0)
            def _():
                finish(g - 1)

            return sums

        zero = jnp.zeros((8, LANES), jnp.float32)
        sums = lax.fori_loop(0, groups, step, (zero, zero) if with_sums else (zero,))
        return sums, functools.partial(finish, groups - 1)

    def collect(stage):
        for g in range(groups):
            for j in range(1, line):
                line_landed(stage, g, j)
        mine = partial[stage, :, pl.ds(z, 1), pl.ds(c, 1)].reshape(blocks, rows, width)
        mine = mine + from_core[stage, :, pl.ds(z, 1)].reshape(blocks, rows, width)
        for j in range(1, line):
            piece = from_line[stage, pl.ds(z_at(j), 1)].reshape(blocks, rows, width)
            mine = mine + piece.astype(jnp.float32)
        for g in range(groups):
            pair_copy(stage, g).wait_send()
            for j in range(1, line):
                line_copy(stage, g, j).wait_send()
        return mine

    def term_copy(stage, j):
        return pltpu.make_async_remote_copy(
            src_ref=term_out.at[stage],
            dst_ref=term_in.at[stage, j],
            send_sem=term_send.at[stage, j],
            recv_sem=term_recv.at[stage, j],
            device_id=(lax.rem(t + j, terms), s),
            device_id_type=MESH,
        )

    def sector_copy(stage, j):
        return pltpu.make_async_remote_copy(
            src_ref=sector_out.at[stage],
            dst_ref=sector_in.at[stage, j],
            send_sem=sector_send.at[stage, j],
            recv_sem=sector_recv.at[stage, j],
            device_id=(t, lax.rem(s + j, sectors)),
            device_id_type=MESH,
        )

    def share_start(stage, tiles):
        for i, tile in enumerate(tiles):
            term_out[stage, i] = tile
        for j in range(1, terms):
            term_copy(stage, j).start()

    def share_turn(stage):
        value = term_out[stage]
        for j in range(1, terms):
            term_copy(stage, j).wait_recv()
            value = value + term_in[stage, j]
        sector_out[stage] = value
        for j in range(1, sectors):
            sector_copy(stage, j).start()

    def share_end(stage):
        value = sector_out[stage]
        for j in range(1, sectors):
            sector_copy(stage, j).wait_recv()
            value = value + sector_in[stage, j]
        for j in range(1, terms):
            term_copy(stage, j).wait_send()
        for j in range(1, sectors):
            sector_copy(stage, j).wait_send()
        return jnp.sum(jnp.sum(value, axis=2, keepdims=True), axis=1, keepdims=True)

    gather(0, wave_region, [0])
    loads[1].wait()
    loads[2].wait()

    sums, last = operate(0, True)
    my_rows = pl.ds(pl.multiple_of(t * rows, rows), rows)
    own = pool[0, pl.ds(s * blocks, blocks), my_rows, :].astype(jnp.float32)
    share_start(0, (sums[0], sums[1], fold(own * own)))
    last()
    share_turn(0)
    first = collect(0)
    first_ref[...] = first
    whole = share_end(0)
    count = float(sectors * blocks * width * width)
    ratio = whole[0:1] / whole[2:3]
    early = jnp.maximum(lax.rsqrt(whole[1:2] / count + epsilon), 1e-18)
    residual = first - ratio * own
    pool[1, pl.ds(s * blocks, blocks), my_rows, :] = (residual * early).astype(jnp.bfloat16)
    zero = jnp.zeros((8, LANES), jnp.float32)
    gather(1, next_region, [0] + [j for i in range(1, line) for j in sorted({i, line - i}) if i <= line - i])
    share_start(1, (fold(residual * residual), zero, zero))

    _, last = operate(1, False)
    last()
    share_turn(1)
    second = collect(1)
    spread = share_end(1)[0:1]
    second_ref[...] = second * (lax.rsqrt(spread / count + epsilon) / early)


def body(dims, wavefunction, left_env, right_env, source, block_size):
    terms, sectors, blocks, bonds, width = dims
    line = terms // 2
    rows = width // terms
    groups = blocks // (2 if blocks % 2 == 0 else 1)
    nx, ny = grid_of(sectors)
    piece = jax.ShapeDtypeStruct((blocks, rows, width), jnp.float32)
    dma = pltpu.SemaphoreType.DMA
    pieces = line * sectors
    sends = line * (nx - 1 + nx * (ny - 1) + sectors) + line
    return pl.pallas_call(
        functools.partial(kernel, dims),
        out_shape=(piece, piece),
        in_specs=[pl.BlockSpec(memory_space=pltpu.SMEM)] * 2
        + [pl.BlockSpec(memory_space=pl.ANY)] * 3,
        out_specs=(pl.BlockSpec(memory_space=pltpu.VMEM),) * 2,
        scratch_shapes=[
            pltpu.VMEM((blocks, width, width), jnp.bfloat16),
            pltpu.VMEM((bonds, blocks, width, width), jnp.bfloat16),
            pltpu.VMEM((bonds, blocks, width, width), jnp.bfloat16),
            pltpu.VMEM((2, sectors * blocks, width, width), jnp.bfloat16),
            pltpu.VMEM((2, blocks, line, 2, rows, width), jnp.float32),
            pltpu.VMEM((2, blocks, line, rows, width), jnp.float32),
            pltpu.VMEM((2, line, blocks, rows, width), jnp.bfloat16),
            pltpu.VMEM((2, line, blocks, rows, width), jnp.bfloat16),
            pltpu.VMEM((2, 3, 8, LANES), jnp.float32),
            pltpu.VMEM((2, terms, 3, 8, LANES), jnp.float32),
            pltpu.VMEM((2, 3, 8, LANES), jnp.float32),
            pltpu.VMEM((2, sectors, 3, 8, LANES), jnp.float32),
            dma((3,)),
            dma((sends,)),
            dma((2, pieces)),
            dma((2, pieces)),
            dma((2, groups)),
            dma((2, groups)),
            dma((2, groups, line)),
            dma((2, groups, line)),
            dma((2, terms)),
            dma((2, terms)),
            dma((2, sectors)),
            dma((2, sectors)),
        ],
        compiler_params=pltpu.CompilerParams(
            collective_id=0, has_side_effects=True, vmem_limit_bytes=60 * 1024 * 1024
        ),
    )(source, block_size, wavefunction, left_env, right_env)


def solution(mesh):
    terms, sectors = mesh.shape["term"], mesh.shape["sector"]

    def local(wavefunction, left_env, right_env, source, block_size):
        blocks, width = wavefunction.shape[0], wavefunction.shape[1]
        dims = (terms, sectors, blocks, source.shape[0], width)
        return body(dims, wavefunction, left_env, right_env, source, block_size)

    placed = (
        P("sector", None, None),
        P("term", "sector", None, None),
        P("term", "sector", None, None),
        P("term", None),
        P("sector", None),
    )
    return jax.shard_map(
        local,
        mesh=mesh,
        in_specs=placed,
        out_specs=(P("sector", "term", None), P("sector", "term", None)),
        check_vma=False,
    )
```

time: 256 us -> 83.7 us (0.33)
  waiting for transfers between devices: 183 us -> 0 us
  Pallas kernels: 0 us -> 78.2 us
  blocking collectives: 19 us -> 0 us
  between operations: 15.9 us -> 0.64 us
  matrix products: 12 us -> 0 us
  other arithmetic: 10.5 us -> 0 us
  local copies, waits for them, and re-layouts: 14.8 us -> 4.58 us
    all_gather x2 -> x0, waiting for transfers between devices: 88.6 us -> none  [fetch_blocks(): pieces = lax.all_gather(masked, 'sector', axis=0, tiled=True)]
    pallas_call x0 -> x1, Pallas kernels: none -> 78.2 us  [body(): pl.pallas_call(functools.partial(kernel, dims), out_shape=(piece, piece),...]
    psum x1 -> x0, waiting for transfers between devices: 62 us -> none  [body(): whole_sum = lax.psum(partial_value, 'term')]
    reduce_scatter x1 -> x0, waiting for transfers between devices: 32.8 us -> none  [body(): lax.psum_scatter(second_partial, 'term', scatter_dimension=1, tiled=True)]
    psum x2 -> x0, blocking collectives: 19 us -> none  [the longest x1 10.4 us: body(): lax.psum((jnp.sum(masked_float * whole_sum), jnp.sum(masked_float * maske...]
    dot_general x4 -> x0, matrix products: 12 us -> none  [the longest x2 9.96 us: apply_operator(): jnp.einsum('bkil,bkml->bkim', half_product, right_env, preferred_element_...]
    unnamed x12 -> x3, local copies, waits for them, and re-layouts: 12.1 us -> 4.58 us
    reduce_sum x2 -> x0, other arithmetic: 5.26 us -> none  [the longest x1 2.64 us: body(): spread = lax.psum(jnp.sum(residual * residual), 'sector')]
  transfers between devices with their start and end apart: 4 -> 0, of which waited for: 4 -> 0; matrix products, arithmetic and copies ran while one was open for 1% -> 0% of each run, Pallas kernels for 0% -> 0%
where the time goes in v1:
time: 83.7 us; the launch traced here: 83.4 us
  Pallas kernels  78.2 us (93%)
  local copies, waits for them, and re-layouts  4.58 us (5%)
    pallas_call x1, Pallas kernels, body(): pl.pallas_call(functools.partial(kernel, dims), out_shape=(piece, piece),...  78.2 us
    unnamed x3, local copies, waits for them, and re-layouts  4.58 us

profile of v1, /device:TPU:0, one launch (start us, length us, event | category | flops | bytes accessed | tf_op | source)
XLA Modules:
  0.0 83.4 jit_solution(8020441710924096409)
XLA Ops:
  0.6 1.4 %copy.7.size_ref = s32[6,2]{1,0:T(8,128)} copy(s32[6,2]{0,1:T(2,128)} %param.9) | data formatting | bytes 96 | tf_op args[4]
  2.0 78.2 %shard_map.68 = (f32[6,32,256]{2,1,0:T(8,128)}, f32[6,32,256]{2,1,0:T(8,128)}) custom-call(s32[3,24]{1,0:T(4,128)} %source_ref.1, s32[6,2]{1,0:T(8,128)} %copy.7.size_ref, bf16[6,256,256]{2,1,0:T(8,128)(2,1)} %wave_hbm.1, bf16[3,6,256,256]{3,2,1,0:T(8,128)(2,1)} %left_hbm.1, bf16[3,6,256,256]{3,2,1,0:T(8,128)(2,1)} %right_hbm.1), custom_call_target="tpu_custom_call" | custom-call | tf_op jit(solution)/shard_map/pallas_call | solution.py:394
  80.2 1.6 %copy.10 = f32[6,32,256]{2,1,0:T(8,128)} copy(f32[6,32,256]{2,1,0:T(8,128)} %get-tuple-element.4) | data formatting | bytes 393216
  81.8 1.6 %copy.11 = f32[6,32,256]{2,1,0:T(8,128)} copy(f32[6,32,256]{2,1,0:T(8,128)} %get-tuple-element.5) | data formatting | bytes 393216

commit v2 on v1

--- a/solution.py
+++ b/solution.py
@@ -10,6 +10,10 @@
 epsilon = 1e-06
 MESH = pl.DeviceIdType.MESH
 LANES = 128
+SHARED = 1
+CUTS = 2
+GROUP = 1
+LAG = 3
 
 
 def grid_of(sector_count):
@@ -65,7 +69,7 @@
     terms, sectors, blocks, bonds, width = dims
     line = terms // 2
     rows = width // terms
-    group = 2 if blocks % 2 == 0 else 1
+    group = GROUP if blocks % GROUP == 0 else 1
     groups = blocks // group
     nx, ny = grid_of(sectors)
     t = lax.axis_index("term")
@@ -109,7 +113,7 @@
     column_at = lax.broadcasted_iota(jnp.int32, (width, width), 1)
 
     def keep_of(k):
-        return (row_at < size_ref[k, 0]) & (column_at < size_ref[k, 1])
+        return (row_at < size_ref[0, k]) & (column_at < size_ref[1, k])
 
     loads[0].wait()
     for k in range(blocks):
@@ -119,18 +123,27 @@
 
     sent = []
 
-    def send(stage, region, slot, target, by_core):
+    def send(stage, region, slot, target, by_core, condition=None):
         number = len(sent)
-        copy = pltpu.make_async_remote_copy(
-            src_ref=region,
-            dst_ref=region,
-            send_sem=send_sem.at[number],
-            recv_sem=(core_sem if by_core else net_sem).at[stage, slot],
-            device_id=target,
-            device_id_type=MESH,
-        )
-        copy.start()
-        sent.append(copy)
+
+        def make():
+            return pltpu.make_async_remote_copy(
+                src_ref=region,
+                dst_ref=region,
+                send_sem=send_sem.at[number],
+                recv_sem=(core_sem if by_core else net_sem).at[stage, slot],
+                device_id=target,
+                device_id_type=MESH,
+            )
+
+        when(condition, lambda: make().start())
+        sent.append((condition, make))
+
+    def when(condition, action):
+        if condition is None:
+            action()
+        else:
+            pl.when(condition)(action)
 
     def arrived(stage, region, slot, by_core):
         pltpu.make_async_remote_copy(
@@ -142,76 +155,145 @@
             device_id_type=MESH,
         ).wait_recv()
 
-    def gather(stage, region_of, z_order):
-        def spread_out(piece, zz, to_first, to_second, to_core):
-            region = region_of(piece, zz, c)
-            slot = zz * sectors + piece
+    def drain():
+        for condition, make in sent:
+            when(condition, lambda make=make: make().wait_send())
+        sent.clear()
+
+    elsewhere = [(a, b) for a in range(nx) for b in range(ny) if a or b]
+
+    def gather_wave():
+        half = width // 2
+        shared = SHARED if line % 2 == 0 and blocks > 2 * SHARED else 0
+        parity = lax.rem(z, 2)
+        mate = z + 1 - 2 * parity
+        common = [parity * shared + i for i in range(shared)]
+        theirs = [(1 - parity) * shared + i for i in range(shared)]
+        alone = list(range(2 * shared, blocks))
+
+        def region_of(piece, k, core):
+            return pool.at[
+                0, piece * blocks + k, pl.ds(pl.multiple_of(core * half, half), half), :
+            ]
+
+        def put(piece, k, to_first=False, to_second=False, to_mate=False, to_core=False):
+            region, slot = region_of(piece, k, c), piece * blocks + k
             if to_second:
                 for b in range(1, ny):
-                    send(stage, region, slot, (t, sector_at(0, b)), False)
+                    send(0, region, slot, (t, sector_at(0, b)), False)
             if to_first:
                 for a in range(1, nx):
-                    send(stage, region, slot, (t, sector_at(a, 0)), False)
+                    send(0, region, slot, (t, sector_at(a, 0)), False)
+            if to_mate:
+                send(0, region, slot, (2 * mate + c, s), False)
             if to_core:
-                send(stage, region, slot, (other, s), True)
-
-        def land(piece, zz):
-            arrived(stage, region_of(piece, zz, c), zz * sectors + piece, False)
-
-        def firsts(j):
-            for a in range(1, nx):
-                piece = sector_at(a, 0)
-                land(piece, z_at(j))
-                spread_out(piece, z_at(j), False, True, True)
-
-        def seconds(j):
-            for a in range(nx):
+                send(0, region, slot, (other, s), True)
+
+        def pass_on(spots, ks, **where):
+            for k in ks:
+                for a, b in spots:
+                    piece = sector_at(a, b)
+                    arrived(0, region_of(piece, k, c), piece * blocks + k, False)
+                    put(piece, k, **where)
+
+        side_one = [(a, 0) for a in range(1, nx)]
+        side_two = [(0, b) for b in range(1, ny)]
+        corners = [(a, b) for a in range(1, nx) for b in range(1, ny)]
+        for k in common:
+            put(s, k, to_first=True, to_second=True)
+        for k in alone:
+            put(s, k, to_first=True)
+        pass_on(side_one, common, to_second=True, to_mate=True, to_core=True)
+        for k in alone:
+            put(s, k, to_second=True)
+        pass_on(side_two, common, to_mate=True, to_core=True)
+        pass_on(side_one, alone[:1], to_second=True, to_core=True)
+        pass_on(corners, common, to_mate=True, to_core=True)
+        pass_on(side_one, alone[1:], to_second=True, to_core=True)
+        pass_on(side_two, alone, to_core=True)
+        pass_on(side_one + side_two, theirs, to_core=True)
+        pass_on(corners, theirs, to_core=True)
+        pass_on(corners, alone, to_core=True)
+        for k in range(blocks):
+            for a, b in elsewhere:
+                piece = sector_at(a, b)
+                arrived(0, region_of(piece, k, 1 - c), piece * blocks + k, True)
+        drain()
+
+    def gather_next():
+        cuts = CUTS if blocks % CUTS == 0 else 1
+        deep = blocks // cuts
+
+        def region_of(piece, zz, q, core):
+            return pool.at[
+                1,
+                pl.ds(piece * blocks + q * deep, deep),
+                pl.ds(pl.multiple_of((2 * zz + core) * rows, rows), rows),
+                :,
+            ]
+
+        def slot_of(piece, zz, q):
+            return (zz * sectors + piece) * cuts + q
+
+        def put(piece, zz, q, valid, to_line=(), to_first=False, to_second=False):
+            region, slot = region_of(piece, zz, q, c), slot_of(piece, zz, q)
+            for step in to_line:
+                inside = (z + step >= 0) & (z + step < line)
+                inside = inside if valid is None else inside & valid
+                send(1, region, slot, (2 * (z + step) + c, s), False, inside)
+            if to_second:
                 for b in range(1, ny):
-                    piece = sector_at(a, b)
-                    land(piece, z_at(j))
-                    spread_out(piece, z_at(j), False, False, True)
-
-        for i, j in enumerate(z_order):
-            if i == 0:
-                for jj in z_order[1:]:
-                    region = region_of(s, z, c)
-                    send(stage, region, z * sectors + s, (2 * z_at(jj) + c, s), False)
-                spread_out(s, z, True, True, len(z_order) > 1)
-            else:
-                land(s, z_at(j))
-                spread_out(s, z_at(j), True, True, True)
-                firsts(z_order[i - 1])
-        firsts(z_order[-1])
-        for j in z_order:
-            seconds(j)
-        for j in z_order:
-            for a in range(nx):
-                for b in range(ny):
-                    if a or b or len(z_order) > 1:
+                    send(1, region, slot, (t, sector_at(0, b)), False, valid)
+            if to_first:
+                for a in range(1, nx):
+                    send(1, region, slot, (t, sector_at(a, 0)), False, valid)
+            send(1, region, slot, (other, s), True, valid)
+
+        def land(piece, zz, q, valid, core=None):
+            spot = c if core is None else core
+            when(
+                valid,
+                lambda: arrived(
+                    1, region_of(piece, zz, q, spot), slot_of(piece, zz, q), core is not None
+                ),
+            )
+
+        def planes(d):
+            if d == 0:
+                return [(z, None, 0)]
+            return [(z - d, z >= d, 1), (z + d, z + d < line, -1)]
+
+        def each(d, spots, q_first=True, **where):
+            for q in range(cuts):
+                for zz, valid, step in planes(d):
+                    for a, b in spots:
                         piece = sector_at(a, b)
-                        arrived(
-                            stage,
-                            region_of(piece, z_at(j), 1 - c),
-                            z_at(j) * sectors + piece,
-                            True,
-                        )
-        for copy in sent:
-            copy.wait_send()
-        sent.clear()
-
-    def wave_region(piece, zz, core):
-        half = width // 2
-        return pool.at[
-            0, pl.ds(piece * blocks, blocks), pl.ds(pl.multiple_of(core * half, half), half), :
-        ]
-
-    def next_region(piece, zz, core):
-        return pool.at[
-            1,
-            pl.ds(piece * blocks, blocks),
-            pl.ds(pl.multiple_of((2 * zz + core) * rows, rows), rows),
-            :,
-        ]
+                        land(piece, zz, q, valid)
+                        put(piece, zz, q, valid, **where)
+
+        def from_line_step(d):
+            for q in range(cuts):
+                for zz, valid, step in planes(d):
+                    land(s, zz, q, valid)
+                    put(s, zz, q, valid, to_line=(step,), to_first=True, to_second=True)
+
+        side_one = [(a, 0) for a in range(1, nx)]
+        rest = [(a, b) for a in range(nx) for b in range(1, ny)]
+        for q in range(cuts):
+            put(s, z, q, None, to_line=(1, -1), to_first=True, to_second=True)
+        for d in range(1, line + 2):
+            if d < line:
+                from_line_step(d)
+            if d - 1 < line:
+                each(d - 1, side_one, to_second=True)
+            if 0 <= d - 2 < line:
+                each(d - 2, rest)
+        for d in range(line):
+            for zz, valid, step in planes(d):
+                for q in range(cuts):
+                    for a, b in [(0, 0)] + elsewhere:
+                        land(sector_at(a, b), zz, q, valid, core=1 - c)
+        drain()
 
     def pair_copy(stage, g):
         span = pl.ds(g * group, group)
@@ -280,15 +362,20 @@
                 partial[stage, k] = total.reshape(line, 2, rows, width)
             pair_copy(stage, g).start()
 
-            @pl.when(g > 0)
+            @pl.when(g >= LAG)
             def _():
-                finish(g - 1)
+                finish(g - LAG)
 
             return sums
 
         zero = jnp.zeros((8, LANES), jnp.float32)
         sums = lax.fori_loop(0, groups, step, (zero, zero) if with_sums else (zero,))
-        return sums, functools.partial(finish, groups - 1)
+
+        def last():
+            for g in range(max(groups - LAG, 0), groups):
+                finish(g)
+
+        return sums, last
 
     def collect(stage):
         for g in range(groups):
@@ -326,8 +413,9 @@
         )
 
     def share_start(stage, tiles):
-        for i, tile in enumerate(tiles):
-            term_out[stage, i] = tile
+        lines = [jnp.sum(tile, axis=0, keepdims=True) for tile in tiles]
+        lines.append(jnp.zeros((8 - len(tiles), LANES), jnp.float32))
+        term_out[stage] = jnp.concatenate(lines, axis=0)
         for j in range(1, terms):
             term_copy(stage, j).start()
 
@@ -349,9 +437,9 @@
             term_copy(stage, j).wait_send()
         for j in range(1, sectors):
             sector_copy(stage, j).wait_send()
-        return jnp.sum(jnp.sum(value, axis=2, keepdims=True), axis=1, keepdims=True)
-
-    gather(0, wave_region, [0])
+        return jnp.sum(value, axis=1, keepdims=True)
+
+    gather_wave()
     loads[1].wait()
     loads[2].wait()
 
@@ -369,9 +457,8 @@
     early = jnp.maximum(lax.rsqrt(whole[1:2] / count + epsilon), 1e-18)
     residual = first - ratio * own
     pool[1, pl.ds(s * blocks, blocks), my_rows, :] = (residual * early).astype(jnp.bfloat16)
-    zero = jnp.zeros((8, LANES), jnp.float32)
-    gather(1, next_region, [0] + [j for i in range(1, line) for j in sorted({i, line - i}) if i <= line - i])
-    share_start(1, (fold(residual * residual), zero, zero))
+    gather_next()
+    share_start(1, (fold(residual * residual),))
 
     _, last = operate(1, False)
     last()
@@ -381,17 +468,22 @@
     second_ref[...] = second * (lax.rsqrt(spread / count + epsilon) / early)
 
 
+def hand_over(first_in, second_in, first_ref, second_ref):
+    first_ref[...] = first_in[...]
+    second_ref[...] = second_in[...]
+
+
 def body(dims, wavefunction, left_env, right_env, source, block_size):
     terms, sectors, blocks, bonds, width = dims
     line = terms // 2
     rows = width // terms
-    groups = blocks // (2 if blocks % 2 == 0 else 1)
+    groups = blocks // (GROUP if blocks % GROUP == 0 else 1)
     nx, ny = grid_of(sectors)
     piece = jax.ShapeDtypeStruct((blocks, rows, width), jnp.float32)
     dma = pltpu.SemaphoreType.DMA
-    pieces = line * sectors
-    sends = line * (nx - 1 + nx * (ny - 1) + sectors) + line
-    return pl.pallas_call(
+    pieces = sectors * max(line * CUTS, blocks)
+    sends = CUTS * 2 * line * (nx + nx * ny + sectors + 2) + blocks * (nx + ny + nx * ny + 2 * sectors)
+    results = pl.pallas_call(
         functools.partial(kernel, dims),
         out_shape=(piece, piece),
         in_specs=[pl.BlockSpec(memory_space=pltpu.SMEM)] * 2
@@ -406,10 +498,10 @@
             pltpu.VMEM((2, blocks, line, rows, width), jnp.float32),
             pltpu.VMEM((2, line, blocks, rows, width), jnp.bfloat16),
             pltpu.VMEM((2, line, blocks, rows, width), jnp.bfloat16),
-            pltpu.VMEM((2, 3, 8, LANES), jnp.float32),
-            pltpu.VMEM((2, terms, 3, 8, LANES), jnp.float32),
-            pltpu.VMEM((2, 3, 8, LANES), jnp.float32),
-            pltpu.VMEM((2, sectors, 3, 8, LANES), jnp.float32),
+            pltpu.VMEM((2, 8, LANES), jnp.float32),
+            pltpu.VMEM((2, terms, 8, LANES), jnp.float32),
+            pltpu.VMEM((2, 8, LANES), jnp.float32),
+            pltpu.VMEM((2, sectors, 8, LANES), jnp.float32),
             dma((3,)),
             dma((sends,)),
             dma((2, pieces)),
@@ -426,7 +518,13 @@
         compiler_params=pltpu.CompilerParams(
             collective_id=0, has_side_effects=True, vmem_limit_bytes=60 * 1024 * 1024
         ),
-    )(source, block_size, wavefunction, left_env, right_env)
+    )(source, block_size.T, wavefunction, left_env, right_env)
+    return pl.pallas_call(
+        hand_over,
+        out_shape=(piece, piece),
+        in_specs=[pl.BlockSpec(memory_space=pltpu.VMEM)] * 2,
+        out_specs=(pl.BlockSpec(memory_space=pltpu.VMEM),) * 2,
+    )(*results)
 
 
 def solution(mesh):

time: 83.7 us -> 71.9 us (0.86)
  Pallas kernels: 78.2 us -> 71.1 us
  local copies, waits for them, and re-layouts: 4.58 us -> 0 us
    pallas_call x1, Pallas kernels: 78.2 us -> 69.3 us  [body(): pl.pallas_call(functools.partial(kernel, dims), out_shape=(piece, piece),...]
    unnamed x3 -> x0, local copies, waits for them, and re-layouts: 4.58 us -> none
    pallas_call x0 -> x1, Pallas kernels: none -> 1.78 us  [body(): pl.pallas_call(hand_over, out_shape=(piece, piece), in_specs=[pl.BlockSpe...]
where the time goes in v2:
time: 71.9 us; the launch traced here: 71.7 us
  Pallas kernels  71.1 us (99%)
    pallas_call x1, Pallas kernels, body(): pl.pallas_call(functools.partial(kernel, dims), out_shape=(piece, piece),...  69.3 us
    pallas_call x1, Pallas kernels, body(): pl.pallas_call(hand_over, out_shape=(piece, piece), in_specs=[pl.BlockSpe...  1.78 us

profile of v2, /device:TPU:0, one launch (start us, length us, event | category | flops | bytes accessed | tf_op | source)
XLA Modules:
  0.0 71.7 jit_solution(13783865104443209835)
XLA Ops:
  0.6 69.3 %shard_map.68 = (f32[6,32,256]{2,1,0:T(8,128)}, f32[6,32,256]{2,1,0:T(8,128)}) custom-call(s32[3,24]{1,0:T(4,128)} %source_ref.1, s32[2,6]{1,0:T(2,128)} %bitcast.1, bf16[6,256,256]{2,1,0:T(8,128)(2,1)} %wave_hbm.1, bf16[3,6,256,256]{3,2,1,0:T(8,128)(2,1)} %left_hbm.1, bf16[3,6,256,256]{3,2,1,0:T(8,128)(2,1)} %right_hbm.1), custom_call_target="tpu_custom_call" | custom-call | tf_op jit(solution)/shard_map/pallas_call | solution.py:486
  69.9 1.8 %shard_map.69 = (f32[6,32,256]{2,1,0:T(8,128)}, f32[6,32,256]{2,1,0:T(8,128)}) custom-call(f32[6,32,256]{2,1,0:T(8,128)} %get-tuple-element.4.first_in, f32[6,32,256]{2,1,0:T(8,128)} %get-tuple-element.5.second_in), custom_call_target="tpu_custom_call" | custom-call | tf_op jit(solution)/shard_map/pallas_call | solution.py:522
